TPU v7x, 128 devices: a whole 4x4x4 slice. The times are simulated.
128 devices in a mesh: gx: 16 (over y, z), gy: 8 (over x, core).
Axes of the slice: x: 4, y: 4, z: 4, core: 2. Of those that a mesh axis runs over, the one named last changes fastest.
Arguments:
- forces: float32 [3, 256, 256, 256], P(None, 'gx', 'gy'), may hold values from -8 to 8
- pressure_prev: float32 [256, 256, 256], P('gx', 'gy'), may hold values from -8 to 8
Outputs:
- pressure: float32 [256, 256, 256], P('gx', 'gy')
- residual: float32 [256, 256, 256], P('gx', 'gy')
All inputs are finite; a program needn't handle non-finite values.
Results may differ from a plain program's by a relative error of at most 0.0003.
Values sent between devices are 32-bit elements; how exact they have to be, the bound alone decides.
A program may use at most 64 MiB of HBM per device.

v0:
```python
import contextlib
import functools

import jax
import jax.numpy as jnp
import numpy as np
from jax import lax
from jax.experimental import pallas as pl
from jax.experimental.pallas import tpu as pltpu
from jax.sharding import PartitionSpec as P

MESH = pl.DeviceIdType.MESH
OMEGA = 0.8
LEVELS = 5
GX, GY = 16, 8
NDEV = GX * GY
BX, BY, NZ = 16, 32, 256
TILES = 5
HIGHEST = lax.Precision.HIGHEST
SCOPES = False
PAUSE = 3600


def steps(distance, size):
    return min(distance, size - distance)


def hops(offset):
    a, b = offset
    return steps(a // 4, 4) + steps(a % 4, 4) + steps(b // 2, 4) + 0.5 * (b % 2)


PARTNERS = sorted(((a, b) for a in range(GX) for b in range(GY) if a or b), key=hops, reverse=True)


def scope(name):
    return jax.named_scope(name) if SCOPES else contextlib.nullcontext()


def spectrum():
    k = np.arange(1, NZ + 1, dtype=np.float64)
    return 4.0 * np.sin(0.5 * np.pi * k / (NZ + 1)) ** 2


def sine_matrix(weight=1.0):
    k = np.arange(1, NZ + 1, dtype=np.float64)
    full = weight * (np.sqrt(2.0 / (NZ + 1)) * np.sin(np.pi * np.outer(k, k) / (NZ + 1)))
    return np.concatenate([full[0::2], full[1::2]]).astype(np.float32)


def eigenvalues():
    rows = np.tile(spectrum().reshape(NDEV, 2), (1, 4))
    return np.broadcast_to(rows[:, :, None], (NDEV, 8, 128)).astype(np.float32)


def iota(axis):
    return lax.broadcasted_iota(jnp.int32, (8, 128), axis)


def shifted_rows(a, edge, up):
    rows = a.shape[0]
    row = lax.broadcasted_iota(jnp.int32, a.shape, 0)
    if up:
        return jnp.where(row == rows - 1, edge, pltpu.roll(a, rows - 1, 0))
    return jnp.where(row == 0, edge, pltpu.roll(a, 1, 0))


def shifted_depth(a, up):
    depth = a.shape[1]
    col = lax.broadcasted_iota(jnp.int32, a.shape, 1)
    if up:
        return jnp.where(col == depth - 1, 0.0, pltpu.roll(a, depth - 1, 1))
    return jnp.where(col == 0, 0.0, pltpu.roll(a, 1, 1))


def transform(x, y, dim):
    return lax.dot_general(x, y, (((dim,), (dim,)), ((), ())), precision=HIGHEST, preferred_element_type=jnp.float32)


def split(x):
    high = x.astype(jnp.bfloat16)
    x = x - high.astype(jnp.float32)
    mid = x.astype(jnp.bfloat16)
    return high, mid, (x - mid.astype(jnp.float32)).astype(jnp.bfloat16)


def product(x, y):
    return lax.dot_general(x, y, (((1,), (0,)), ((), ())), preferred_element_type=jnp.float32)


def fence():
    pl.delay(1)


class Lanes:
    def __init__(self):
        gx = lax.rem(iota(1), GX)
        self.first, self.last = gx == 0, gx == GX - 1
        self.sub = iota(0)

    def from_left(self, v):
        return jnp.where(self.first, pltpu.roll(v, 128 - (GX - 1), 1), pltpu.roll(v, 1, 1))

    def from_right(self, v):
        return jnp.where(self.last, pltpu.roll(v, GX - 1, 1), pltpu.roll(v, 127, 1))

    def from_below(self, v):
        return pltpu.roll(v, GX, 1)

    def from_above(self, v):
        return pltpu.roll(v, 128 - GX, 1)


class Field:
    def __init__(self, level, ref=None):
        self.level, self.ref, self.held = level, ref, {}
        self.nx, self.ny = BX >> level, max(1, 4 >> level)
        self.step = max(1, (1 << level) // 4)

    def cells(self):
        return [(x, y) for x in range(self.nx) for y in range(self.ny)]

    def get(self, x, y):
        return self.held[x, y] if self.ref is None else self.ref[x, y]

    def put(self, x, y, value):
        if self.ref is None:
            self.held[x, y] = value
        else:
            self.ref[x, y] = value

    def beside(self, x, y, lanes):
        step = self.step
        left = self.get(x - 1, y) if x > 0 else lanes.from_left(self.get(self.nx - 1, y))
        right = self.get(x + 1, y) if x < self.nx - 1 else lanes.from_right(self.get(0, y))
        if y > 0:
            below = self.get(x, y - 1)
        else:
            below = pltpu.roll(self.get(x, self.ny - 1), step, 0)
            below = jnp.where(lanes.sub < step, lanes.from_below(below), below)
        if y < self.ny - 1:
            above = self.get(x, y + 1)
        else:
            above = pltpu.roll(self.get(x, 0), 8 - step, 0)
            above = jnp.where(lanes.sub >= 8 - step, lanes.from_above(above), above)
        return (left + right) + (below + above)


def weights(level):
    w = 0.25**level
    return w, OMEGA / (4.0 * w + 2.0)


def sweep(source, f, target, lam, lanes):
    w, c = weights(source.level)
    keep = 1.0 - c * (4.0 * w + lam)
    for x, y in source.cells():
        beside = source.beside(x, y, lanes)
        target.put(x, y, keep * source.get(x, y) + ((c * w) * beside + c * f.get(x, y)))


def first_two(f, target, lam, lanes):
    w, c = weights(f.level)
    keep = c * (2.0 - c * (4.0 * w + lam))
    for x, y in f.cells():
        target.put(x, y, keep * f.get(x, y) + (c * c * w) * f.beside(x, y, lanes))


def coarsen(source, f, coarse, lam, lanes):
    w, _ = weights(source.level)

    def rest(x, y):
        own = source.get(x, y)
        return f.get(x, y) - (w * (4.0 * own - source.beside(x, y, lanes)) + lam * own)

    for x, y in coarse.cells():
        if source.ny > 1:
            total = (rest(2 * x, 2 * y) + rest(2 * x + 1, 2 * y)) + (rest(2 * x, 2 * y + 1) + rest(2 * x + 1, 2 * y + 1))
        else:
            step = source.step
            both = rest(2 * x, y) + rest(2 * x + 1, y)
            even = lax.rem(lanes.sub // step, 2) == 0
            total = both + jnp.where(even, pltpu.roll(both, 8 - step, 0), pltpu.roll(both, step, 0))
        coarse.put(x, y, 0.25 * total)


def correct(target, e):
    for x, y in target.cells():
        target.put(x, y, target.get(x, y) + e.get(x // 2, y // 2 if target.ny > 1 else 0))


def coarsest(f, lam, lanes):
    level = f.level
    _, c = weights(level)
    own = f.get(0, 0)
    total = jnp.broadcast_to(jnp.sum(own, axis=1, keepdims=True), (8, 128))
    total = total + pltpu.roll(total, 4, 0)
    total = total + pltpu.roll(total, 2, 0)
    total = total + pltpu.roll(total, 1, 0)
    u = (total * (1.0 / 1024.0)) / lam
    decay = (1.0 - c * lam) * (1.0 - c * lam)
    v = Field(level)
    first_two(f, v, lam, lanes)
    for _ in range(2):
        new = Field(level)
        sweep(v, f, new, lam, lanes)
        v = new
    v.put(0, 0, v.get(0, 0) + (decay * decay) * u)
    return v


def kernel(
    f_hbm, p_hbm, s_hbm, st_hbm, lam_hbm,
    e_ref, r_ref, p_ref,
    f_ref, s_ref, st_ref, lam_ref, g_ref, o_ref, basis,
    send, recv, reply, back, w_ref, row_ref, f0, a0, b0, f1, a1, b1,
    in_sem, s_sem, r_sem,
):
    gx, gy = lax.axis_index("gx"), lax.axis_index("gy")
    me = gy * GX + gx
    loads = [
        pltpu.make_async_copy(source, target, in_sem.at[n])
        for n, (source, target) in enumerate(
            ((f_hbm, f_ref), (p_hbm, p_ref), (s_hbm, s_ref), (st_hbm, st_ref), (lam_hbm.at[me], lam_ref))
        )
    ]
    for load in loads:
        load.start()

    to_x = [lax.rem(gx + a, GX) for a in range(GX)]

    to_y = [lax.rem(gy + b, GY) for b in range(GY)]

    def partners(visit, order=PARTNERS):
        for a, b in order:
            visit(to_x[a], to_y[b])

    barrier = pltpu.get_barrier_semaphore()
    with scope("greet"):
        partners(lambda x, y: pl.semaphore_signal(barrier, inc=1, device_id=(x, y), device_id_type=MESH))
    with scope("load"):
        for load in loads:
            load.wait()

    with scope("stage_a"):
        g_ref[0:32] = f_ref[0, BX - 1] + p_ref[BX - 1]
        g_ref[32:64] = p_ref[0]
        g_ref[96:128] = jnp.zeros((32, NZ), jnp.float32)
        for i in range(BX):
            p, fx, fy, fz = p_ref[i], f_ref[0, i], f_ref[1, i], f_ref[2, i]
            r = shifted_depth(fz, False) - ((fx + fy + fz) + 4.0 * p)
            r = r + (shifted_rows(fy + p, 0.0, False) + shifted_rows(p, 0.0, True))
            if i > 0:
                r = r + (f_ref[0, i - 1] + p_ref[i - 1])
            if i < BX - 1:
                r = r + p_ref[i + 1]
            r_ref[i] = r
            g_ref[64 + i] = f_ref[1, i, BY - 1] + p_ref[i, BY - 1]
            g_ref[80 + i] = p_ref[i, 0]

    with scope("dst"):
        for t in range(4):
            rows = r_ref[4 * t : 4 * t + 4].reshape(128, NZ)
            flat = p_ref[4 * t : 4 * t + 4].reshape(128, NZ)
            o_ref[t] = transform(s_ref[...], rows, 1) + transform(st_ref[...], flat, 1)
        o_ref[4] = transform(s_ref[...], g_ref[...], 1)
    with scope("pack"):
        for k in range(2):
            for t in range(TILES):
                send[k, pl.ds(t, NDEV, stride=TILES), :] = o_ref[t, k * NDEV : (k + 1) * NDEV]

    with scope("basis"):
        for k in range(2):
            high, mid, low = split(s_ref[k * NDEV : (k + 1) * NDEV])
            for n, (first, second) in enumerate(((high, high), (mid, mid), (low, high))):
                basis[k, n, 0:NDEV] = first
                basis[k, n, NDEV : 2 * NDEV] = second

    with scope("barrier"):
        pl.semaphore_wait(barrier, NDEV - 1)

    def start_all_to_all(source, target, which, low=0, high=NDEV):
        mine = target.at[pl.ds(me * TILES, TILES)]

        def visit(x, y):
            pltpu.make_async_remote_copy(
                source.at[pl.ds((y * GX + x) * TILES, TILES)], mine, s_sem.at[which], r_sem.at[which],
                device_id=(x, y), device_id_type=MESH,
            ).start()

        partners(visit, PARTNERS[low:high])
        if low == 0:
            target[pl.ds(me * TILES, TILES), :] = source[pl.ds(me * TILES, TILES), :]

    def wait_all(ref, sem):
        most = ref.at[pl.ds(0, (NDEV - 1) * TILES)]
        pltpu.make_async_copy(most, most, sem).wait()

    with scope("a2a_1_start"):
        start_all_to_all(send.at[0], recv.at[0], 0)
        pl.delay(PAUSE)
        start_all_to_all(send.at[1], recv.at[1], 1)

    lanes = Lanes()

    def unpack(k):
        w = w_ref.at[k]
        for n in range(TILES):
            w[n] = recv[k, pl.ds(n, NDEV, stride=TILES), :].T
        for half in range(2):
            at = 8 * half
            row_ref[k, at : at + 8] = lanes.from_below(w[4, 64 + at : 72 + at])
            row_ref[k, 16 + at : 24 + at] = lanes.from_above(w[4, 80 + at : 88 + at])
        for x in range(BX):
            t, x4 = divmod(x, 4)
            for y in range(4):
                value = w[t, pl.ds(32 * x4 + y, 8, stride=4), :]
                if x == 0:
                    value = value + lanes.from_left(w[4, pl.ds(y, 8, stride=4), :])
                if x == BX - 1:
                    value = value + lanes.from_right(w[4, pl.ds(32 + y, 8, stride=4), :])
                if y == 0:
                    value = value + jnp.where(lanes.sub == 0, row_ref[k, x : x + 1], 0.0)
                if y == 3:
                    value = value + jnp.where(lanes.sub == 7, row_ref[k, 16 + x : 17 + x], 0.0)
                f0[k, x, y] = value

    lams = [jnp.broadcast_to(lam_ref[k : k + 1], (8, 128)) for k in range(2)]

    fields = [[(Field(0, f0.at[k]), Field(0, a0.at[k]), Field(0, b0.at[k])) for k in range(2)],
              [(Field(1, f1.at[k]), Field(1, a1.at[k]), Field(1, b1.at[k])) for k in range(2)]]

    def small(f, lam):
        level = f.level
        if level == LEVELS - 1:
            return coarsest(f, lam, lanes)
        v, coarse = Field(level), Field(level + 1)
        first_two(f, v, lam, lanes)
        coarsen(v, f, coarse, lam, lanes)
        correct(v, small(coarse, lam))
        for _ in range(2):
            new = Field(level)
            sweep(v, f, new, lam, lanes)
            v = new
        return v

    def cycle(k, level, first):
        f, a, b = fields[level][k]
        lam = lams[k]
        smooth = [
            (f"sweep_{level}", lambda: sweep(b, f, a, lam, lanes)),
            (f"sweep_{level}", lambda: sweep(a, f, b, lam, lanes)),
        ]
        passes = [(f"first_two_{level}", lambda: first_two(f, b, lam, lanes))] if first else list(smooth)
        if level == 0:
            passes.append(("coarsen_0", lambda: coarsen(b, f, fields[1][k][0], lam, lanes)))
            passes += cycle(k, 1, True)
            passes.append(("correct_0", lambda: correct(b, fields[1][k][2])))
        else:
            def inner():
                coarse = Field(2)
                coarsen(b, f, coarse, lam, lanes)
                correct(b, small(coarse, lam))

            passes.append((f"inner_{level}", inner))
        return passes + smooth

    def run(*lists):
        for together in zip(*lists, strict=True):
            with scope("+".join(name for name, _ in together)):
                for _, step in together:
                    step()
            fence()

    def gather_edges(k):
        w = w_ref.at[k]
        edge = w.at[4]
        for y in range(4):
            low = edge[pl.ds(y, 8, stride=4), :] + b0[k, BX - 1, y]
            high = edge[pl.ds(32 + y, 8, stride=4), :] + b0[k, 0, y]
            edge[pl.ds(y, 8, stride=4), :] = lanes.from_left(low)
            edge[pl.ds(32 + y, 8, stride=4), :] = lanes.from_right(high)
        for x in range(BX):
            edge[64 + x : 65 + x, :] = row_ref[k, x : x + 1] + lanes.from_below(b0[k, x, 3])[7:8]
            edge[80 + x : 81 + x, :] = row_ref[k, 16 + x : 17 + x] + lanes.from_above(b0[k, x, 0])[0:1]
            t, x4 = divmod(x, 4)
            for y in range(4):
                w[t, pl.ds(32 * x4 + y, 8, stride=4), :] = b0[k, x, y]

    def turn(k):
        for n in range(TILES):
            reply[k, pl.ds(n, NDEV, stride=TILES), :] = w_ref[k, n].T

    with scope("a2a_1_wait_0"):
        wait_all(recv.at[0], r_sem.at[0])
    run([("unpack", lambda: unpack(0))] + cycle(0, 0, True))
    run(cycle(0, 0, False) + [("gather", lambda: gather_edges(0)), ("turn", lambda: turn(0))])
    with scope("a2a_1_wait_1"):
        wait_all(recv.at[1], r_sem.at[1])
    early = [("unpack", lambda: unpack(1))] + cycle(1, 0, True)
    cuts = (0, 25, 42, 60, 72, NDEV - 1)
    sends = [
        ("send", functools.partial(start_all_to_all, reply.at[0], back.at[0], 2, low, high))
        for low, high in zip(cuts[:-1], cuts[1:])
    ]
    run(early[: len(sends)], sends)
    run(early[len(sends) :] + cycle(1, 0, False) + [("gather", lambda: gather_edges(1)), ("turn", lambda: turn(1))])
    with scope("a2a_2_start"):
        start_all_to_all(reply.at[1], back.at[1], 3)

    for k in range(2):
        with scope(f"a2a_2_wait_{k}"):
            wait_all(back.at[k], r_sem.at[2 + k])
        with scope("idst"):
            turned = jnp.concatenate([back[k, pl.ds(t, NDEV, stride=TILES), :].T for t in range(TILES)], axis=0)
            high, mid, low = split(turned)
            both, outer = jnp.concatenate([high, mid], axis=1), jnp.concatenate([high, low], axis=1)
            part = product(both, basis[k, 0]) + (product(both, basis[k, 1]) + product(outer, basis[k, 2]))
            e_ref[...] = part if k == 0 else e_ref[...] + part

    with scope("drain"):
        for k in range(2):
            wait_all(send.at[k], s_sem.at[k])
            wait_all(reply.at[k], s_sem.at[2 + k])


def finish(e_ref, r_ref, p_ref, pressure_hbm, residual_hbm, pressure_ref, residual_ref, sem):
    def plane(i):
        return e_ref[32 * i : 32 * i + 32]

    stores = []
    for i in range(BX):
        e = plane(i)
        p = p_ref[i] + e
        pressure_ref[i] = p
        r = r_ref[i] - 4.0 * e + (shifted_depth(p, False) + shifted_depth(p, True) - 2.0 * p)
        r = r + (shifted_rows(e, e_ref[576 + i : 577 + i], False) + shifted_rows(e, e_ref[592 + i : 593 + i], True))
        r = r + (plane(i - 1) if i > 0 else e_ref[512:544])
        r = r + (plane(i + 1) if i < BX - 1 else e_ref[544:576])
        residual_ref[i] = r
        if i % 4 == 3:
            part = pl.ds(i - 3, 4)
            for n, (source, target) in enumerate(((pressure_ref, pressure_hbm), (residual_ref, residual_hbm))):
                store = pltpu.make_async_copy(source.at[part], target.at[part], sem.at[n, i // 4])
                store.start()
                stores.append(store)
    for store in stores:
        store.wait()


def on_device(forces, pressure_prev):
    block = (BX, BY, NZ)
    anywhere = pl.BlockSpec(memory_space=pl.ANY)

    def vmem(*shape):
        return pltpu.VMEM(shape, jnp.float32)

    e, r, p = pl.pallas_call(
        kernel,
        out_shape=(vmem(TILES * 128, NZ), vmem(*block), vmem(*block)),
        in_specs=[anywhere] * 5,
        out_specs=(pl.BlockSpec(memory_space=pltpu.VMEM),) * 3,
        scratch_shapes=[
            vmem(3, *block), vmem(NZ, NZ), vmem(NZ, NZ), vmem(8, 128), vmem(128, NZ), vmem(TILES, NZ, 128), pltpu.VMEM((2, 3, NZ, NZ), jnp.bfloat16),
            *[vmem(2, NDEV * TILES, 128)] * 4, vmem(2, TILES, 128, 128), vmem(2, 32, 128),
            *[vmem(2, 16, 4, 8, 128)] * 3, *[vmem(2, 8, 2, 8, 128)] * 3,
            pltpu.SemaphoreType.DMA((5,)),
            pltpu.SemaphoreType.DMA((4,)),
            pltpu.SemaphoreType.DMA((4,)),
        ],
        compiler_params=pltpu.CompilerParams(collective_id=0, has_side_effects=True),
        name="poisson",
    )(
        forces,
        pressure_prev,
        jnp.asarray(sine_matrix()),
        jnp.asarray(sine_matrix(-spectrum()[:, None])),
        jnp.asarray(eigenvalues()),
    )
    e, r, p = (pltpu.with_memory_space_constraint(x, pltpu.VMEM) for x in (e, r, p))
    return pl.pallas_call(
        finish,
        out_shape=(jax.ShapeDtypeStruct(block, jnp.float32), jax.ShapeDtypeStruct(block, jnp.float32)),
        in_specs=[pl.BlockSpec(memory_space=pltpu.VMEM)] * 3,
        out_specs=(anywhere, anywhere),
        scratch_shapes=[vmem(*block), vmem(*block), pltpu.SemaphoreType.DMA((2, 4))],
        name="finish",
    )(e, r, p)


def solution(mesh):
    return jax.shard_map(
        on_device,
        mesh=mesh,
        in_specs=(P(None, "gx", "gy", None), P("gx", "gy", None)),
        out_specs=(P("gx", "gy", None), P("gx", "gy", None)),
        check_vma=False,
    )
```

profile of v0, /device:TPU:1, one launch (start us, length us, event | category | flops | bytes accessed | tf_op | source)
XLA Modules:
  0.0 36.7 jit_solution(16218143831402094442)
XLA Ops:
  0.6 34.9 %poisson.1 = (f32[640,256]{1,0:T(8,128)S(1)}, f32[16,32,256]{2,1,0:T(8,128)S(1)}, f32[16,32,256]{2,1,0:T(8,128)S(1)}) custom-call(f32[3,16,32,256]{3,2,1,0:T(8,128)} %f_hbm.1, f32[16,32,256]{2,1,0:T(8,128)} %p_hbm.1, f32[256,256]{1,0:T(8,128)} %constant.6.clone.s_hbm, f32[256,256]{1,0:T(8,128)} %constant.7.clone.st_hbm, f32[128,8,128]{2,1,0:T(8,128)} %constant.8.clone.lam_hbm), custom_call_target="tpu_custom_call" | custom-call | tf_op jit(solution)/shard_map/poisson/pallas_call | solution.py:458
  35.5 1.2 %finish.1 = (f32[16,32,256]{2,1,0:T(8,128)}, f32[16,32,256]{2,1,0:T(8,128)}) custom-call(f32[640,256]{1,0:T(8,128)S(1)} %get-tuple-element.5.e_ref, f32[16,32,256]{2,1,0:T(8,128)S(1)} %get-tuple-element.6.r_ref, f32[16,32,256]{2,1,0:T(8,128)S(1)} %get-tuple-element.7.p_ref), custom_call_target="tpu_custom_call" | custom-call | tf_op jit(solution)/shard_map/finish/pallas_call | solution.py:481
where the time goes:
time: 36.8 us; the launch traced here: 36.7 us
  Pallas kernels  36 us (98%)
  between operations  0.64 us (2%)
    pallas_call x1, Pallas kernels, on_device(): pl.pallas_call(kernel, out_shape=(vmem(TILES * 128, NZ), vmem(*block), vm...  34.9 us
    pallas_call x1, Pallas kernels, on_device(): pl.pallas_call(finish, out_shape=(jax.ShapeDtypeStruct(block, jnp.float32...  1.16 us

commit v1 on v0

--- a/solution.py
+++ b/solution.py
@@ -404,8 +404,9 @@
         for low, high in zip(cuts[:-1], cuts[1:])
     ]
     run(early[: len(sends)], sends)
-    run(early[len(sends) :] + cycle(1, 0, False) + [("gather", lambda: gather_edges(1)), ("turn", lambda: turn(1))])
-    with scope("a2a_2_start"):
+    run(early[len(sends) :] + cycle(1, 0, False) + [("gather", lambda: gather_edges(1))])
+    with scope("turn+send"):
+        turn(1)
         start_all_to_all(reply.at[1], back.at[1], 3)
 
     for k in range(2):
@@ -438,10 +439,10 @@
         r = r + (plane(i - 1) if i > 0 else e_ref[512:544])
         r = r + (plane(i + 1) if i < BX - 1 else e_ref[544:576])
         residual_ref[i] = r
-        if i % 4 == 3:
-            part = pl.ds(i - 3, 4)
+        if i % 2 == 1:
+            part = pl.ds(i - 1, 2)
             for n, (source, target) in enumerate(((pressure_ref, pressure_hbm), (residual_ref, residual_hbm))):
-                store = pltpu.make_async_copy(source.at[part], target.at[part], sem.at[n, i // 4])
+                store = pltpu.make_async_copy(source.at[part], target.at[part], sem.at[n, i // 2])
                 store.start()
                 stores.append(store)
     for store in stores:
@@ -483,7 +484,7 @@
         out_shape=(jax.ShapeDtypeStruct(block, jnp.float32), jax.ShapeDtypeStruct(block, jnp.float32)),
         in_specs=[pl.BlockSpec(memory_space=pltpu.VMEM)] * 3,
         out_specs=(anywhere, anywhere),
-        scratch_shapes=[vmem(*block), vmem(*block), pltpu.SemaphoreType.DMA((2, 4))],
+        scratch_shapes=[vmem(*block), vmem(*block), pltpu.SemaphoreType.DMA((2, 8))],
         name="finish",
     )(e, r, p)
 

time: 36.8 us -> 36.8 us (level)
  no operation moved by 1% of the time
where the time goes in v1:
time: 36.8 us; the launch traced here: 36.7 us
  Pallas kernels  36.1 us (98%)
  between operations  0.64 us (2%)
    pallas_call x1, Pallas kernels, on_device(): pl.pallas_call(kernel, out_shape=(vmem(TILES * 128, NZ), vmem(*block), vm...  34.9 us
    pallas_call x1, Pallas kernels, on_device(): pl.pallas_call(finish, out_shape=(jax.ShapeDtypeStruct(block, jnp.float32...  1.2 us

profile of v1, /device:TPU:1, one launch (start us, length us, event | category | flops | bytes accessed | tf_op | source)
XLA Modules:
  0.0 36.7 jit_solution(4747997841906222814)
XLA Ops:
  0.6 34.9 %poisson.1 = (f32[640,256]{1,0:T(8,128)S(1)}, f32[16,32,256]{2,1,0:T(8,128)S(1)}, f32[16,32,256]{2,1,0:T(8,128)S(1)}) custom-call(f32[3,16,32,256]{3,2,1,0:T(8,128)} %f_hbm.1, f32[16,32,256]{2,1,0:T(8,128)} %p_hbm.1, f32[256,256]{1,0:T(8,128)} %constant.6.clone.s_hbm, f32[256,256]{1,0:T(8,128)} %constant.7.clone.st_hbm, f32[128,8,128]{2,1,0:T(8,128)} %constant.8.clone.lam_hbm), custom_call_target="tpu_custom_call" | custom-call | tf_op jit(solution)/shard_map/poisson/pallas_call | solution.py:459
  35.5 1.2 %finish.1 = (f32[16,32,256]{2,1,0:T(8,128)}, f32[16,32,256]{2,1,0:T(8,128)}) custom-call(f32[640,256]{1,0:T(8,128)S(1)} %get-tuple-element.5.e_ref, f32[16,32,256]{2,1,0:T(8,128)S(1)} %get-tuple-element.6.r_ref, f32[16,32,256]{2,1,0:T(8,128)S(1)} %get-tuple-element.7.p_ref), custom_call_target="tpu_custom_call" | custom-call | tf_op jit(solution)/shard_map/finish/pallas_call | solution.py:482
